TPU v7x, 64 devices: a 2x2x8 block of a 4x4x8 slice. The times are simulated.
64 devices in a mesh: dp: 4 (over x, y), sp: 16 (over z, core).
Axes of the slice: x: 2, y: 2, z: 8, core: 2. Of those that a mesh axis runs over, the one named last changes fastest.
The devices are a block of a 4x4x8 slice.
Arguments:
- x_tok: bfloat16 [131072, 1024], P(('dp', 'sp')), parts along dimension 0
- doc_start: int32 [131072], P(('dp', 'sp')), parts along dimension 0
- w_q: bfloat16 [1024, 8, 128], replicated
- w_k: bfloat16 [1024, 8, 128], replicated
- w_v: bfloat16 [1024, 8, 128], replicated
- w_o: bfloat16 [8, 128, 1024], replicated
- dy_tok: bfloat16 [131072, 1024], P(('dp', 'sp')), parts along dimension 0
Outputs:
- output 1: bfloat16 [131072, 1024], P(('dp', 'sp')), parts along dimension 0
- output 2: bfloat16 [131072, 1024], P(('dp', 'sp')), parts along dimension 0
- output 3: float32 [4096, 8, 128], P('dp'), parts along dimension 0
- output 4: float32 [4096, 8, 128], P('dp'), parts along dimension 0
- output 5: float32 [4096, 8, 128], P('dp'), parts along dimension 0
- output 6: float32 [32, 128, 1024], P('dp'), parts along dimension 0
There are 4 independent parts. A program takes and returns all parts, laid end to end along the dimension named above; an argument that names none is the same for every part.
All inputs are finite; a program needn't handle non-finite values.
Results may differ from a plain program's by a relative error of at most 0.00174767.
Values are sent between devices in bfloat16 or wider.
A program may use at most 768 MiB of HBM per device.

v0:
```python
import functools
import math

import jax
import jax.numpy as jnp
from jax import lax
from jax.experimental import pallas as pl
from jax.experimental.pallas import tpu as pltpu
from jax.sharding import PartitionSpec as P

F32 = jnp.float32
BF16 = jnp.bfloat16
MESH = pl.DeviceIdType.MESH
TILE = 256


def dot(lhs, rhs, lhs_dim, rhs_dim):
    return lax.dot_general(lhs, rhs, (((lhs_dim,), (rhs_dim,)), ((), ())), preferred_element_type=F32)


ROWS = 512
GROUP = 2


def front_kernel(size, heads, bounds_ref, gate_ref, x_ref, dy_ref, wq_ref, wk_ref, wv_ref, wo_ref,
                 q_ref, k_ref, v_ref, do_ref, out_ref,
                 mn, inbox, outbox, partner, partner_gate, fwd,
                 in_sem, out_sem, fwd_send, fwd_recv, pair_send, pair_recv, gate_send, gate_recv):
    toks = x_ref.shape[0]
    width = q_ref.shape[2]
    first_pos = bounds_ref[0]
    last_pos = bounds_ref[1]
    step = pl.program_id(0)
    me = lax.axis_index('sp')
    core = lax.rem(me, 2)
    chip = me // 2
    chips = size // 2
    peer = me + 1 - 2 * core
    ahead = 4 * core - 2
    nxt = lax.rem(me + ahead + size, size)
    prv = lax.rem(me - ahead + size, size)
    rank = core * chip + (1 - core) * (chips - 1 - chip)

    def copy(src, dst, send, recv, dev):
        return pltpu.make_async_remote_copy(src_ref=src, dst_ref=dst, send_sem=send, recv_sem=recv,
                                            device_id={'sp': dev}, device_id_type=MESH)

    def give(h):
        return copy(mn.at[core, h], partner.at[h], pair_send.at[h], pair_recv.at[h], peer)

    def hop(h):
        return copy(outbox.at[h], inbox.at[h], out_sem.at[h], in_sem.at[h], nxt)

    def hand(h):
        return copy(inbox.at[h], fwd.at[h], fwd_send.at[h], fwd_recv.at[h], peer)

    give_gate = copy(gate_ref, partner_gate, gate_send.at[0], gate_recv.at[0], peer)

    @pl.when(step == 0)
    def _():
        barrier = pltpu.get_barrier_semaphore()
        for other in (peer, nxt, prv):
            pl.semaphore_signal(barrier, inc=1, device_id={'sp': other}, device_id_type=MESH)
        pl.semaphore_wait(barrier, 3)
        give_gate.start()

        @pl.when(rank == 0)
        def _():
            inbox[...] = jnp.zeros_like(inbox)

        give_gate.wait()

    def relay(h):
        give(h).wait()

        @pl.when(rank > 0)
        def _():
            hop(h).wait_recv()

        state = partner_gate[0:1, :] * inbox[h] + partner[h]

        @pl.when(rank < chips - 1)
        def _():
            outbox[h] = gate_ref[0:1, :] * state + mn[1 - core, h]
            hop(h).start()

        hand(h).start()
        out_ref[1 - core, h] = state.astype(BF16)

    def run_slot(index):
        head = (2 * step + index - 2 - rank) // 2 * GROUP
        due = 2 * step + index - 2 - rank

        @pl.when((due >= 0) & (lax.rem(due + 2 * size, 2) == 0) & (head < heads))
        def _():
            for n in range(GROUP):
                relay(head + n)

    def project(rows_ref, w_ref, w_dim, out):
        for i in range(toks // ROWS):
            row = pl.ds(i * ROWS, ROWS)
            block = dot(rows_ref[row, :], w_ref[...], 1, w_dim).astype(BF16)
            for n in range(GROUP):
                out[n, row] = block[:, n * width:(n + 1) * width]

    pos = lax.broadcasted_iota(jnp.int32, (toks, width), 0)

    @pl.when(step * GROUP < heads)
    def _():
        project(x_ref, wv_ref, 0, v_ref)
        project(x_ref, wk_ref, 0, k_ref)
        for n in range(GROUP):
            v_tail = jnp.where(pos >= last_pos, v_ref[n].astype(F32), 0.0).astype(BF16)
            mn[0, step * GROUP + n] = dot(k_ref[n], v_tail, 0, 0)

    run_slot(0)

    @pl.when(step * GROUP < heads)
    def _():
        project(dy_ref, wo_ref, 1, do_ref)
        project(x_ref, wq_ref, 0, q_ref)
        for n in range(GROUP):
            do_head = jnp.where(pos < first_pos, do_ref[n].astype(F32), 0.0).astype(BF16)
            mn[1, step * GROUP + n] = dot(q_ref[n], do_head, 0, 0)
        for n in range(GROUP):
            give(step * GROUP + n).start()

    run_slot(1)

    @pl.when(step == pl.num_programs(0) - 1)
    def _():
        for h in range(heads):
            hand(h).wait()
            out_ref[core, h] = fwd[h].astype(BF16)

            @pl.when(rank < chips - 1)
            def _():
                hop(h).wait_send()


def front(size, bounds, gate, x, dy, w_q, w_k, w_v, w_o, heads):
    toks, model = x.shape
    width = model // heads
    groups = heads // GROUP
    chips = size // 2
    wide = GROUP * width
    once = pl.Buffered(1)
    last = groups - 1
    vmem = pl.BlockSpec(memory_space=pltpu.VMEM)
    whole = pl.BlockSpec((toks, model), lambda g: (0, 0), pipeline_mode=once)
    cols = pl.BlockSpec((model, wide), lambda g: (0, jnp.minimum(g, last)))
    rows = pl.BlockSpec((wide, model), lambda g: (jnp.minimum(g, last), 0))
    out = pl.BlockSpec((GROUP, toks, width), lambda g: (jnp.minimum(g, last), 0, 0))
    buf = pltpu.VMEM((heads, width, width), F32)
    dma = pltpu.SemaphoreType.DMA
    proj = jax.ShapeDtypeStruct((heads, toks, width), BF16)
    return pl.pallas_call(
        functools.partial(front_kernel, size, heads),
        grid=((2 * groups + chips + 1) // 2,),
        in_specs=[pl.BlockSpec(memory_space=pltpu.SMEM), pl.BlockSpec((8, width), lambda g: (0, 0)),
                  whole, whole, cols, cols, cols, rows],
        out_specs=[out] * 4 + [pl.BlockSpec((2, heads, width, width), lambda g: (0, 0, 0, 0))],
        out_shape=[proj] * 4 + [jax.ShapeDtypeStruct((2, heads, width, width), BF16)],
        scratch_shapes=[pltpu.VMEM((2, heads, width, width), F32), buf, buf, buf, pltpu.VMEM((8, width), F32), buf]
        + [dma((heads,))] * 6 + [dma((1,))] * 2,
        compiler_params=pltpu.CompilerParams(collective_id=0, has_side_effects=True,
                                             vmem_limit_bytes=56 * 2**20,
                                             dimension_semantics=('arbitrary',)),
        cost_estimate=pl.CostEstimate(flops=8 * toks * model * model, bytes_accessed=12 * toks * model,
                                      transcendentals=0),
        name='front',
    )(bounds, gate, x, dy, w_q, w_k, w_v, w_o)


SLOTS = 4
LAST = 8


def attn_kernel(scale, heads, size, bounds_ref, start_ref, q_ref, k_ref, v_ref, do_ref, st_ref, x_ref, dy_ref,
                o_ref, dq_ref, dk_ref, dv_ref, grad_ref,
                score, part, partner, ring, total, give_send, give_recv, ring_send, ring_recv,
                out_sem, out_send, out_recv):
    toks, width = q_ref.shape[1:]
    tiles = toks // TILE
    first_pos = bounds_ref[0]
    last_pos = bounds_ref[1]
    step = pl.program_id(0)
    me = lax.axis_index('sp')
    core = lax.rem(me, 2)
    chip = me // 2
    chips = size // 2
    peer = me + 1 - 2 * core
    sides = (lax.rem(me + 2, size), lax.rem(me + size - 2, size))
    far = chips // 2

    def copy(src, dst, send, recv, dev):
        return pltpu.make_async_remote_copy(src_ref=src, dst_ref=dst, send_sem=send, recv_sem=recv,
                                            device_id={'sp': dev}, device_id_type=MESH)

    @pl.when(step == 0)
    def _():
        barrier = pltpu.get_barrier_semaphore()
        for other in (peer,) + sides:
            pl.semaphore_signal(barrier, inc=1, device_id={'sp': other}, device_id_type=MESH)
        pl.semaphore_wait(barrier, 3)

    def give(head):
        slot = lax.rem(head, 3)
        return copy(part.at[slot, 1 - core], partner.at[head], give_send.at[slot], give_recv.at[slot], peer)

    def hops(mat, side):
        return far if side == mat else chips - 1 - far

    def sent(mat, side, event):
        count = hops(mat, side)
        return 0 <= event < count or far <= event < far + count

    def chunk(mat, side, event):
        sign = 1 - 2 * side
        if event < far:
            return lax.rem(chip + sign * (hops(mat, side) - event) + chips, chips)
        return lax.rem(chip - sign * (event - far) + chips, chips)

    def ship(head, mat, side, event):
        which = chunk(mat, side, event)
        if event == 0:
            src = partner.at[head, mat, which]
        elif event < far:
            src = ring.at[head, mat, side, event - 1]
        else:
            src = total.at[head, mat, which]
        dst = ring.at[head, mat, side, event] if event < far else total.at[head, mat, which]
        slot = lax.rem(head, 4)
        return copy(src, dst, ring_send.at[slot, mat, side, event], ring_recv.at[slot, mat, side, event], sides[side])

    def outputs(head):
        src = total.at[head]
        dst = grad_ref.at[core, head]
        return (pltpu.make_async_copy(src, dst, out_sem.at[head]),
                copy(src, dst, out_send.at[head], out_recv.at[head], peer))

    def run_event(head, event):
        slot = lax.rem(head, 3)
        if event == 0:
            give(head).wait()
        for mat in range(2):
            for side in ((mat, 1 - mat) if event != far else (1 - mat, mat)):
                if sent(mat, side, event - 1):
                    ship(head, mat, side, event - 1).wait()
                if sent(mat, side, event) and event < far:
                    which = chunk(mat, side, event)
                    if event == 0:
                        partner[head, mat, which] = partner[head, mat, which] + part[slot, core, mat, which]
                    else:
                        ring[head, mat, side, event - 1] = (ring[head, mat, side, event - 1]
                                                            + (part[slot, core, mat, which] + partner[head, mat, which]))
                    ship(head, mat, side, event).start()
                elif sent(mat, side, event) and event > far:
                    ship(head, mat, side, event).start()
            if event == far:
                total[head, mat, chip] = ((ring[head, mat, mat, far - 1] + ring[head, mat, 1 - mat, chips - 2 - far])
                                          + (part[slot, core, mat, chip] + partner[head, mat, chip]))
                ship(head, mat, mat, event).start()
                ship(head, mat, 1 - mat, event).start()
        if event == LAST:
            for out in outputs(head):
                out.start()

    def run_slot(index):
        for back in range(2, -1, -1):
            event = SLOTS * back + index
            if event <= LAST:
                head = step - 1 - back

                @pl.when((head >= 0) & (head < heads))
                def _():
                    run_event(head, event)

    def compute(body):
        pl.when(step < heads)(body)

    def scores(lhs_ref, rhs_ref):
        for i in range(tiles):
            row = pl.ds(i * TILE, TILE)
            left = pl.ds(0, (i + 1) * TILE)
            shape = (TILE, (i + 1) * TILE)
            start = jnp.concatenate([start_ref[row, :]] * (shape[1] // width), axis=1)
            u_pos = lax.broadcasted_iota(jnp.int32, shape, 1)
            seen = (u_pos >= start) & (u_pos <= lax.broadcasted_iota(jnp.int32, shape, 0) + i * TILE)
            score[row, left] = jnp.where(seen, dot(lhs_ref[0, row], rhs_ref[0, left], 1, 1) * scale, 0.0).astype(BF16)

    fwd = st_ref[0, 0]
    rev = st_ref[1, 0]

    def strips(row_ref, row_left, row_add, row_dim, col_ref, col_left, col_add, col_dim):
        for i in range(tiles):
            row = pl.ds(i * TILE, TILE)
            left = pl.ds(0, (i + 1) * TILE)
            below = pl.ds(i * TILE, toks - i * TILE)
            t_pos = lax.broadcasted_iota(jnp.int32, (TILE, width), 0) + i * TILE
            row_ref[0, row] = (dot(score[row, left], row_left[0, left], 1, 0)
                               + jnp.where(t_pos < first_pos, dot(row_add[0, row], fwd, 1, row_dim) * scale, 0.0)
                               ).astype(BF16)
            col_ref[0, row] = (dot(score[below, row], col_left[0, below], 0, 0)
                               + jnp.where(t_pos >= last_pos, dot(col_add[0, row], rev, 1, col_dim) * scale, 0.0)
                               ).astype(BF16)

    @compute
    def _():
        scores(q_ref, k_ref)

    run_slot(0)

    @compute
    def _():
        strips(o_ref, v_ref, q_ref, 0, dv_ref, do_ref, k_ref, 0)

    run_slot(1)

    @compute
    def _():
        scores(do_ref, v_ref)

    run_slot(2)

    @compute
    def _():
        strips(dq_ref, k_ref, do_ref, 1, dk_ref, q_ref, v_ref, 1)

    run_slot(3)

    @compute
    def _():
        slot = lax.rem(step, 3)
        rows = jnp.concatenate([dq_ref[0], dk_ref[0], dv_ref[0]], axis=1)
        cut = 2 * width
        for j in range(x_ref.shape[1] // cut):
            col = pl.ds(j * cut, cut)
            grads = dot(rows, x_ref[:, col], 0, 0)
            grad_o = dot(o_ref[0], dy_ref[:, col], 0, 0)
            for n in range(2):
                for mat in range(3):
                    block = grads[mat * width:(mat + 1) * width, n * width:(n + 1) * width]
                    part[slot, mat // 2, mat % 2, 2 * j + n] = block.T
                part[slot, 1, 1, 2 * j + n] = grad_o[:, n * width:(n + 1) * width]
        give(step).start()

    @pl.when(step == heads + 2)
    def _():
        for head in range(heads):
            for out in outputs(head):
                out.wait()


def attention(scale, size, bounds, start, q, k, v, do, states, x, dy):
    heads, toks, width = q.shape
    model = x.shape[1]
    chips = size // 2
    chunk = model // chips
    once = pl.Buffered(1)
    row = pl.BlockSpec((1, toks, width), lambda h: (jnp.minimum(h, heads - 1), 0, 0))
    whole = pl.BlockSpec((toks, model), lambda h: (0, 0), pipeline_mode=once)
    out = jax.ShapeDtypeStruct(q.shape, BF16)
    block = (chips, chunk, width)
    dma = pltpu.SemaphoreType.DMA
    return pl.pallas_call(
        functools.partial(attn_kernel, scale, heads, size),
        grid=(heads + 3,),
        in_specs=[pl.BlockSpec(memory_space=pltpu.SMEM),
                  pl.BlockSpec((toks, width), lambda h: (0, 0), pipeline_mode=once),
                  row, row, row, row,
                  pl.BlockSpec((2, 1, width, width), lambda h: (0, jnp.minimum(h, heads - 1), 0, 0)),
                  whole, whole],
        out_specs=[row] * 4 + [pl.BlockSpec(memory_space=pl.ANY)],
        out_shape=[out] * 4 + [jax.ShapeDtypeStruct((2, heads, 2) + block, F32)],
        scratch_shapes=[pltpu.VMEM((toks, toks), BF16),
                        pltpu.VMEM((3, 2, 2) + block, F32),
                        pltpu.VMEM((heads, 2) + block, F32),
                        pltpu.VMEM((heads, 2, 2, chips // 2, chunk, width), F32),
                        pltpu.VMEM((heads, 2) + block, F32),
                        dma((3,)), dma((3,)), dma((4, 2, 2, 8)), dma((4, 2, 2, 8)),
                        dma((heads,)), dma((heads,)), dma((heads,))],
        compiler_params=pltpu.CompilerParams(collective_id=1, has_side_effects=True,
                                             vmem_limit_bytes=62 * 2**20,
                                             dimension_semantics=('arbitrary',)),
        cost_estimate=pl.CostEstimate(flops=6 * heads * toks * toks * width, bytes_accessed=16 * heads * toks * width,
                                      transcendentals=0),
        name='attention',
    )(bounds, start, q, k, v, do, states, x, dy)


def finish_kernel(o_ref, dq_ref, dk_ref, dv_ref, wq_ref, wk_ref, wv_ref, wo_ref, grad_ref,
                  y_ref, dx_ref, gq_ref, gk_ref, gv_ref, go_ref):
    heads, rows, width = o_ref.shape
    chunks, chunk = grad_ref.shape[3:5]

    def flat(ref):
        return jnp.concatenate([ref[h] for h in range(heads)], axis=1)

    y_ref[...] = dot(flat(o_ref), wo_ref[...], 1, 0).astype(BF16)
    for n, out in enumerate((gq_ref, gk_ref, gv_ref)):
        for j in range(chunks):
            for h in range(heads):
                out[j * chunk:(j + 1) * chunk, h, :] = grad_ref[n // 2, h, n % 2, j]
    for j in range(chunks):
        for h in range(heads):
            go_ref[h, :, j * chunk:(j + 1) * chunk] = grad_ref[1, h, 1, j]
    dx_ref[...] = (dot(flat(dq_ref), wq_ref[...], 1, 1) + dot(flat(dk_ref), wk_ref[...], 1, 1)
                   + dot(flat(dv_ref), wv_ref[...], 1, 1)).astype(BF16)


def finish(out, dq, dk, dv, w_q, w_k, w_v, w_o, grads):
    heads, toks, width = out.shape
    model = w_o.shape[1]
    tiles = toks // ROWS
    chunks, chunk = grads.shape[3:5]
    per = chunks // tiles
    part = pl.BlockSpec((heads, ROWS, width), lambda i: (0, i, 0))
    whole = pl.BlockSpec((model, model), lambda i: (0, 0), pipeline_mode=pl.Buffered(1))
    row = pl.BlockSpec((ROWS, model), lambda i: (i, 0))
    gin = pl.BlockSpec((2, heads, 2, per, chunk, width), lambda i: (0, 0, 0, i, 0, 0))
    gout = pl.BlockSpec((per * chunk, heads, width), lambda i: (i, 0, 0))
    gout_o = pl.BlockSpec((heads, width, per * chunk), lambda i: (0, 0, i))
    act = jax.ShapeDtypeStruct((toks, model), BF16)
    grad = jax.ShapeDtypeStruct((model, heads, width), F32)
    return pl.pallas_call(
        finish_kernel,
        grid=(tiles,),
        in_specs=[part] * 4 + [whole] * 4 + [gin],
        out_specs=[row, row, gout, gout, gout, gout_o],
        out_shape=[act, act, grad, grad, grad, jax.ShapeDtypeStruct((heads, width, model), F32)],
        compiler_params=pltpu.CompilerParams(vmem_limit_bytes=60 * 2**20),
        cost_estimate=pl.CostEstimate(flops=8 * toks * model * model, bytes_accessed=64 * 2**20, transcendentals=0),
        name='finish',
    )(out, dq, dk, dv, w_q, w_k, w_v, w_o, grads)


def solution(mesh):
    seq_devs = mesh.shape['sp']

    def device_body(x_loc, flag_loc, w_q, w_k, w_v, w_o, dy_loc):
        toks = x_loc.shape[0]
        width = w_q.shape[2]
        scale = 1.0 / (math.sqrt(width) * toks)
        pos = jnp.arange(toks, dtype=jnp.int32)
        is_start = flag_loc > 0
        first_pos = jnp.min(jnp.where(is_start, pos, toks))
        last_pos = jnp.max(jnp.where(is_start, pos, -1))
        bounds = jnp.stack([first_pos, last_pos]).astype(jnp.int32)
        start = lax.cummax(jnp.where(is_start, pos, 0))
        start = jnp.broadcast_to(start[:, None], (toks, width))
        gate = jnp.broadcast_to((last_pos < 0).astype(F32), (8, width))

        heads = w_q.shape[1]
        flat_q, flat_k, flat_v = [w.reshape(w.shape[0], heads * width) for w in (w_q, w_k, w_v)]
        flat_o = w_o.reshape(heads * width, w_o.shape[2])
        q, k, v, do, states = front(seq_devs, bounds, gate, x_loc, dy_loc, flat_q, flat_k, flat_v, flat_o, heads)
        out, dq, dk, dv, grads = attention(scale, seq_devs, bounds, start, q, k, v, do, states, x_loc, dy_loc)
        return finish(out, dq, dk, dv, flat_q, flat_k, flat_v, flat_o, grads)

    row_spec = P(('dp', 'sp'), None)
    flag_spec = P(('dp', 'sp'))
    w_spec = P(None, None, None)
    dw_spec = P('dp', None, None)
    return jax.shard_map(device_body, mesh=mesh,
                         in_specs=(row_spec, flag_spec, w_spec, w_spec, w_spec, w_spec, row_spec),
                         out_specs=(row_spec, row_spec, dw_spec, dw_spec, dw_spec, dw_spec),
                         check_vma=False)
```

profile of v0, /device:TPU:21, one launch (start us, length us, event | category | flops | bytes accessed | tf_op | source)
XLA Modules:
  0.0 331.7 jit_solution(7381346122178340588)
XLA Ops:
  0.6 0.0 copy-start
  0.6 0.8 select_bitcast_fusion
  1.5 0.3 reduce-window.9
  1.8 0.6 select_reduce_fusion.1
  3.1 1.9 pad_add_fusion.bounds_ref
  4.9 0.6 broadcast_in_dim.20.gate_ref
  5.5 0.1 slice.9
  5.6 0.0 copy-start.1
  5.7 0.1 slice_reduce_fusion
  5.8 0.1 maximum_bitcast_fusion
  5.8 1.3 broadcast_in_dim.19.start_ref
  7.2 3.5 %copy.19 = bf16[128,8,8,128]{3,1,2,0:T(8,128)(2,1)} copy(bf16[128,8,8,128]{3,2,1,0:T(8,128)(2,1)} %bitcast.17) | data formatting | bytes 4194304
  10.7 0.0 copy-done
  10.7 0.0 copy-done.1
  10.7 3.3 copy_bitcast_fusion
  14.0 65.4 %front.1 = (bf16[8,2048,128]{2,1,0:T(8,128)(2,1)}, bf16[8,2048,128]{2,1,0:T(8,128)(2,1)}, bf16[8,2048,128]{2,1,0:T(8,128)(2,1)}, bf16[8,2048,128]{2,1,0:T(8,128)(2,1)}, bf16[2,8,128,128]{3,2,1,0:T(8,128)(2,1)}) custom-call(s32[2]{0:T(128)} %pad_add_fusion.bounds_ref, f32[8,128]{1,0:T(8,128)} %broadcast_in_dim.20.gate_ref, bf16[2048,1024]{1,0:T(8,128)(2,1)} %x_ref.3, ...), custom_call_target="tpu_custom_call" | custom-call | flops 17179869184 | bytes 25165824 | tf_op jit(solution)/shard_map/front/pallas_call | solution.py:157
  79.4 220.0 %attention.1 = (bf16[8,2048,128]{2,1,0:T(8,128)(2,1)}, bf16[8,2048,128]{2,1,0:T(8,128)(2,1)}, bf16[8,2048,128]{2,1,0:T(8,128)(2,1)}, bf16[8,2048,128]{2,1,0:T(8,128)(2,1)}, f32[2,8,2,8,128,128]{5,4,3,2,1,0:T(8,128)}) custom-call(s32[2]{0:T(128)} %pad_add_fusion.bounds_ref, s32[2048,128]{1,0:T(8,128)} %broadcast_in_dim.19.start_ref, ...), custom_call_target="tpu_custom_call" | custom-call | flops 25769803776 | bytes 33554432 | tf_op jit(solution)/shard_map/attention/pallas_call | solution.py:366
  299.4 32.2 %finish.1 = (bf16[2048,1024]{1,0:T(8,128)(2,1)}, bf16[2048,1024]{1,0:T(8,128)(2,1)}, f32[1024,8,128]{2,1,0:T(8,128)}, f32[1024,8,128]{2,1,0:T(8,128)}, f32[1024,8,128]{2,1,0:T(8,128)}, /*index=5*/f32[8,128,1024]{2,1,0:T(8,128)}) custom-call(bf16[8,2048,128]{2,1,0:T(8,128)(2,1)} %get-tuple-element.21.o_ref, bf16[8,2048,128]{2,1,0:T(8,128)(2,1)} %get-tuple-element.22.dq_ref, ...), custom_call_target="tpu_custom_call" | custom-call | flops 17179869184 | bytes 67108864 | tf_op jit(solution)/shard_map/finish/pallas_call | solution.py:426
  (1 shorter events, 0.0 us)
Async XLA Ops:
  0.6 10.1 %copy-start = (bf16[1024,8,128]{2,1,0:T(8,128)(2,1)S(1)}, bf16[1024,8,128]{2,1,0:T(8,128)(2,1)}, u32[]{:S(2)}) copy-start(bf16[1024,8,128]{2,1,0:T(8,128)(2,1)} %param.11) | copy-start | bytes 6291460
  5.6 5.0 %copy-start.1 = (bf16[1024,8,128]{2,1,0:T(8,128)(2,1)S(1)}, bf16[1024,8,128]{2,1,0:T(8,128)(2,1)}, u32[]{:S(2)}) copy-start(bf16[1024,8,128]{2,1,0:T(8,128)(2,1)} %param.10) | copy-start | bytes 6291460
where the time goes:
time: 332 us
  Pallas kernels  318 us (96%)
  local copies, waits for them, and re-layouts  8.89 us (3%)
  other arithmetic  3.76 us (1%)
    pallas_call x1, Pallas kernels, attention(): pl.pallas_call(functools.partial(attn_kernel, scale, heads, size), grid=(...  220 us
    pallas_call x1, Pallas kernels, front(): pl.pallas_call(functools.partial(front_kernel, size, heads), grid=((2 * g...  65.4 us
    pallas_call x1, Pallas kernels, finish(): pl.pallas_call(finish_kernel, grid=(tiles,), in_specs=[part] * 4 + [whole...  32.2 us

commit v1 on v0

--- a/solution.py
+++ b/solution.py
@@ -172,7 +172,7 @@
     )(bounds, gate, x, dy, w_q, w_k, w_v, w_o)
 
 
-SLOTS = 4
+SLOTS = 3
 LAST = 8
 
 
@@ -305,44 +305,45 @@
                                + jnp.where(t_pos >= last_pos, dot(col_add[0, row], rev, 1, col_dim) * scale, 0.0)
                                ).astype(BF16)
 
-    @compute
-    def _():
-        scores(q_ref, k_ref)
-
-    run_slot(0)
-
-    @compute
-    def _():
-        strips(o_ref, v_ref, q_ref, 0, dv_ref, do_ref, k_ref, 0)
-
-    run_slot(1)
-
-    @compute
-    def _():
-        scores(do_ref, v_ref)
-
-    run_slot(2)
-
-    @compute
-    def _():
-        strips(dq_ref, k_ref, do_ref, 1, dk_ref, q_ref, v_ref, 1)
-
-    run_slot(3)
-
-    @compute
-    def _():
+    def grads(cols):
         slot = lax.rem(step, 3)
         rows = jnp.concatenate([dq_ref[0], dk_ref[0], dv_ref[0]], axis=1)
         cut = 2 * width
-        for j in range(x_ref.shape[1] // cut):
+        for j in cols:
             col = pl.ds(j * cut, cut)
-            grads = dot(rows, x_ref[:, col], 0, 0)
+            grad_rows = dot(rows, x_ref[:, col], 0, 0)
             grad_o = dot(o_ref[0], dy_ref[:, col], 0, 0)
             for n in range(2):
                 for mat in range(3):
-                    block = grads[mat * width:(mat + 1) * width, n * width:(n + 1) * width]
+                    block = grad_rows[mat * width:(mat + 1) * width, n * width:(n + 1) * width]
                     part[slot, mat // 2, mat % 2, 2 * j + n] = block.T
                 part[slot, 1, 1, 2 * j + n] = grad_o[:, n * width:(n + 1) * width]
+
+    cuts = x_ref.shape[1] // (2 * width)
+
+    @compute
+    def _():
+        scores(q_ref, k_ref)
+
+    run_slot(0)
+
+    @compute
+    def _():
+        strips(o_ref, v_ref, q_ref, 0, dv_ref, do_ref, k_ref, 0)
+        scores(do_ref, v_ref)
+
+    run_slot(1)
+
+    @compute
+    def _():
+        strips(dq_ref, k_ref, do_ref, 1, dk_ref, q_ref, v_ref, 1)
+        grads(range(cuts // 2))
+
+    run_slot(2)
+
+    @compute
+    def _():
+        grads(range(cuts // 2, cuts))
         give(step).start()
 
     @pl.when(step == heads + 2)
@@ -400,8 +401,7 @@
     y_ref[...] = dot(flat(o_ref), wo_ref[...], 1, 0).astype(BF16)
     for n, out in enumerate((gq_ref, gk_ref, gv_ref)):
         for j in range(chunks):
-            for h in range(heads):
-                out[j * chunk:(j + 1) * chunk, h, :] = grad_ref[n // 2, h, n % 2, j]
+            out[j * chunk:(j + 1) * chunk] = jnp.transpose(grad_ref[n // 2, :, n % 2, j], (1, 0, 2))
     for j in range(chunks):
         for h in range(heads):
             go_ref[h, :, j * chunk:(j + 1) * chunk] = grad_ref[1, h, 1, j]
@@ -412,12 +412,12 @@
 def finish(out, dq, dk, dv, w_q, w_k, w_v, w_o, grads):
     heads, toks, width = out.shape
     model = w_o.shape[1]
-    tiles = toks // ROWS
+    tiles = toks // TILE
     chunks, chunk = grads.shape[3:5]
     per = chunks // tiles
-    part = pl.BlockSpec((heads, ROWS, width), lambda i: (0, i, 0))
+    part = pl.BlockSpec((heads, TILE, width), lambda i: (0, i, 0))
     whole = pl.BlockSpec((model, model), lambda i: (0, 0), pipeline_mode=pl.Buffered(1))
-    row = pl.BlockSpec((ROWS, model), lambda i: (i, 0))
+    row = pl.BlockSpec((TILE, model), lambda i: (i, 0))
     gin = pl.BlockSpec((2, heads, 2, per, chunk, width), lambda i: (0, 0, 0, i, 0, 0))
     gout = pl.BlockSpec((per * chunk, heads, width), lambda i: (i, 0, 0))
     gout_o = pl.BlockSpec((heads, width, per * chunk), lambda i: (0, 0, i))

time: 332 us -> 306 us (0.922)
  Pallas kernels: 318 us -> 292 us
    pallas_call x1, Pallas kernels: 220 us -> 198 us  [attention(): pl.pallas_call(functools.partial(attn_kernel, scale, heads, size), grid=(...]
    pallas_call x1, Pallas kernels: 32.2 us -> 28.3 us  [finish(): pl.pallas_call(finish_kernel, grid=(tiles,), in_specs=[part] * 4 + [whole...]
where the time goes in v1:
time: 306 us
  Pallas kernels  292 us (95%)
  local copies, waits for them, and re-layouts  8.89 us (3%)
  other arithmetic  3.76 us (1%)
    pallas_call x1, Pallas kernels, attention(): pl.pallas_call(functools.partial(attn_kernel, scale, heads, size), grid=(...  198 us
    pallas_call x1, Pallas kernels, front(): pl.pallas_call(functools.partial(front_kernel, size, heads), grid=((2 * g...  65.4 us
    pallas_call x1, Pallas kernels, finish(): pl.pallas_call(finish_kernel, grid=(tiles,), in_specs=[part] * 4 + [whole...  28.3 us

profile of v1, /device:TPU:21, one launch (start us, length us, event | category | flops | bytes accessed | tf_op | source)
XLA Modules:
  0.0 305.7 jit_solution(14865916894821757989)
XLA Ops:
  0.6 0.0 copy-start
  0.6 0.8 select_bitcast_fusion
  1.5 0.3 reduce-window.9
  1.8 0.6 select_reduce_fusion.1
  3.1 1.9 pad_add_fusion.bounds_ref
  4.9 0.6 broadcast_in_dim.20.gate_ref
  5.5 0.1 slice.9
  5.6 0.0 copy-start.1
  5.7 0.1 slice_reduce_fusion
  5.8 0.1 maximum_bitcast_fusion
  5.8 1.3 broadcast_in_dim.19.start_ref
  7.2 3.5 %copy.19 = bf16[128,8,8,128]{3,1,2,0:T(8,128)(2,1)} copy(bf16[128,8,8,128]{3,2,1,0:T(8,128)(2,1)} %bitcast.17) | data formatting | bytes 4194304
  10.7 0.0 copy-done
  10.7 0.0 copy-done.1
  10.7 3.3 %copy_bitcast_fusion = (bf16[1024,1024]{1,0:T(8,128)(2,1)}, bf16[1024,1024]{1,0:T(8,128)(2,1)}) fusion(bf16[128,8,8,128]{3,2,1,0:T(8,128)(2,1)S(1)} %bitcast.20, bf16[128,8,8,128]{3,2,1,0:T(8,128)(2,1)S(1)} %bitcast.21), kind=kLoop, calls=%fused_computation | loop fusion | bytes 8388608 | tf_op jit(solution)/shard_map/reshape | solution.py:455
  14.0 65.4 %front.1 = (bf16[8,2048,128]{2,1,0:T(8,128)(2,1)}, bf16[8,2048,128]{2,1,0:T(8,128)(2,1)}, bf16[8,2048,128]{2,1,0:T(8,128)(2,1)}, bf16[8,2048,128]{2,1,0:T(8,128)(2,1)}, bf16[2,8,128,128]{3,2,1,0:T(8,128)(2,1)}) custom-call(s32[2]{0:T(128)} %pad_add_fusion.bounds_ref, f32[8,128]{1,0:T(8,128)} %broadcast_in_dim.20.gate_ref, bf16[2048,1024]{1,0:T(8,128)(2,1)} %x_ref.3, ...), custom_call_target="tpu_custom_call" | custom-call | flops 17179869184 | bytes 25165824 | tf_op jit(solution)/shard_map/front/pallas_call | solution.py:157
  79.4 197.9 %attention.1 = (bf16[8,2048,128]{2,1,0:T(8,128)(2,1)}, bf16[8,2048,128]{2,1,0:T(8,128)(2,1)}, bf16[8,2048,128]{2,1,0:T(8,128)(2,1)}, bf16[8,2048,128]{2,1,0:T(8,128)(2,1)}, f32[2,8,2,8,128,128]{5,4,3,2,1,0:T(8,128)}) custom-call(s32[2]{0:T(128)} %pad_add_fusion.bounds_ref, s32[2048,128]{1,0:T(8,128)} %broadcast_in_dim.19.start_ref, ...), custom_call_target="tpu_custom_call" | custom-call | flops 25769803776 | bytes 33554432 | tf_op jit(solution)/shard_map/attention/pallas_call | solution.py:367
  277.2 28.3 %finish.1 = (bf16[2048,1024]{1,0:T(8,128)(2,1)}, bf16[2048,1024]{1,0:T(8,128)(2,1)}, f32[1024,8,128]{2,1,0:T(8,128)}, f32[1024,8,128]{2,1,0:T(8,128)}, f32[1024,8,128]{2,1,0:T(8,128)}, /*index=5*/f32[8,128,1024]{2,1,0:T(8,128)}) custom-call(bf16[8,2048,128]{2,1,0:T(8,128)(2,1)} %get-tuple-element.21.o_ref, bf16[8,2048,128]{2,1,0:T(8,128)(2,1)} %get-tuple-element.22.dq_ref, ...), custom_call_target="tpu_custom_call" | custom-call | flops 17179869184 | bytes 67108864 | tf_op jit(solution)/shard_map/finish/pallas_call | solution.py:426
  (1 shorter events, 0.0 us)
Async XLA Ops:
  0.6 10.1 %copy-start = (bf16[1024,8,128]{2,1,0:T(8,128)(2,1)S(1)}, bf16[1024,8,128]{2,1,0:T(8,128)(2,1)}, u32[]{:S(2)}) copy-start(bf16[1024,8,128]{2,1,0:T(8,128)(2,1)} %param.11) | copy-start | bytes 6291460
  5.6 5.0 %copy-start.1 = (bf16[1024,8,128]{2,1,0:T(8,128)(2,1)S(1)}, bf16[1024,8,128]{2,1,0:T(8,128)(2,1)}, u32[]{:S(2)}) copy-start(bf16[1024,8,128]{2,1,0:T(8,128)(2,1)} %param.10) | copy-start | bytes 6291460
